TPU v7x, 32 devices: a whole 2x2x4 slice. The times are simulated.
32 devices in a mesh: param: 16 (over z, y, x), sensor: 2 (over core).
Axes of the slice: x: 2, y: 2, z: 4, core: 2. Of those that a mesh axis runs over, the one named last changes fastest.
Arguments:
- data: float32 [16, 512, 420], P(None, ('sensor', 'param')), may hold values from -6 to 6
- spectra: float32 [2, 512, 64, 421], P(None, 'sensor', 'param'), may hold values from -2 to 2
Outputs:
- gradient: float32 [16, 64, 420], P(None, 'param')
- rms: float32 [16], replicated
All inputs are finite; a program needn't handle non-finite values.
Results may differ from a plain program's by a relative error of at most 0.0003.
Values sent between devices are 32-bit elements; how exact they have to be, the bound alone decides.
A program may use at most 128 MiB of HBM per device.

v0:
```python
import math
import jax
import jax.numpy as jnp
from jax import lax
from jax.sharding import PartitionSpec as P


def spectral_tables(steps):
    length = 2 * steps
    freqs = steps + 1
    times = lax.broadcasted_iota(jnp.int32, (steps, freqs), 0)
    bins = lax.broadcasted_iota(jnp.int32, (steps, freqs), 1)
    phase = 2.0 * math.pi / length * (times * bins % length).astype(jnp.float32)
    forward = jnp.concatenate([jnp.cos(phase), -jnp.sin(phase)], axis=1)
    weight = jnp.where((bins == 0) | (bins == steps), 1.0, 2.0) / length
    backward = jnp.concatenate([(weight * jnp.cos(phase)).T, (-weight * jnp.sin(phase)).T], axis=0)
    return (forward, backward)


def to_spectrum(series, forward):
    vectors, sensors, steps = series.shape
    flat = jnp.dot(
        series.reshape(vectors * sensors, steps),
        forward,
        precision=lax.Precision.HIGHEST,
        preferred_element_type=jnp.float32,
    )
    return flat.reshape(vectors, sensors, forward.shape[1])


def contract(kernel, spectrum):
    return jnp.einsum(
        "spf,rsf->rpf",
        kernel,
        spectrum,
        precision=lax.Precision.HIGHEST,
        preferred_element_type=jnp.float32,
    )


def body(data, spectra):
    steps = data.shape[2]
    freqs = steps + 1
    forward, backward = spectral_tables(steps)
    whole = to_spectrum(lax.all_gather(data, "param", axis=1, tiled=True), forward)
    real_part = whole[..., :freqs]
    imag_part = whole[..., freqs:]
    kernel_re = spectra[0]
    kernel_im = spectra[1]
    out_re = contract(kernel_re, real_part) + contract(kernel_im, imag_part)
    out_im = contract(kernel_re, imag_part) - contract(kernel_im, real_part)
    vectors, points = (out_re.shape[0], out_re.shape[1])
    stacked = jnp.concatenate([out_re, out_im], axis=2).reshape(vectors * points, 2 * freqs)
    partial_field = jnp.dot(
        stacked, backward, precision=lax.Precision.HIGHEST, preferred_element_type=jnp.float32
    ).reshape(vectors, points, steps)
    count = points * lax.axis_size("param") * steps
    share = lax.psum_scatter(partial_field, "sensor", scatter_dimension=0, tiled=True)
    squares = lax.psum(jnp.sum(share * share, axis=(1, 2)), "param")
    scale = jnp.sqrt(squares / count + 1e-06)
    normalized = share / scale[:, None, None]
    gradient, rms_all = (
        lax.all_gather(normalized, "sensor", axis=0, tiled=True),
        lax.all_gather(scale, "sensor", axis=0, tiled=True),
    )
    return (gradient, rms_all)


def solution(mesh):
    in_specs = (P(None, ("sensor", "param"), None), P(None, "sensor", "param", None))
    out_specs = (P(None, "param", None), P())
    return jax.shard_map(body, mesh=mesh, in_specs=in_specs, out_specs=out_specs, check_vma=False)
```

profile of v0, /device:TPU:0, one launch (start us, length us, event | category | flops | bytes accessed | tf_op | source)
XLA Modules:
  0.0 326.7 jit_solution(8645191133042081712)
XLA Ops:
  7.2 0.0 copy-start
  7.2 0.0 all-gather.2.cloned.1.call-start
  7.2 0.7 all-gather.2.cloned.1.call-update
  7.9 0.0 reduce-scatter.2.cloned.1.call-start
  8.0 4.5 %sine_negate_fusion = (f32[420,421]{1,0:T(8,128)}, f32[420,421]{1,0:T(8,128)}) fusion(), kind=kLoop, calls=%fused_computation.39 | loop fusion | flops 1768200 | bytes 1414560 | tf_op jit(solution)/shard_map/neg | solution.py:14
  12.5 4.6 %sine_multiply_fusion = (f32[421,420]{0,1:T(8,128)}, f32[421,420]{0,1:T(8,128)}) fusion(f32[421]{0:T(512)S(1)} %fusion.42, f32[421]{0:T(512)S(1)} %select_multiply_fusion), kind=kLoop, calls=%fused_computation.34 | loop fusion | flops 1945020 | bytes 1417928 | tf_op jit(solution)/shard_map/mul | solution.py:16
  17.0 0.0 copy-done
  17.0 1.5 fusion.73
  18.5 1.5 fusion.71
  20.0 1.5 fusion.75
  21.6 1.5 fusion.77
  23.1 102.6 %all-gather.2.cloned.1.call-done = f32[16,256,420]{2,1,0:T(8,128)} async-done(((f32[16,16,420]{2,1,0:T(8,128)}), f32[16,256,420]{2,1,0:T(8,128)}) %all-gather.2.cloned.1.call-update) | async-done | bytes 6881296 | tf_op jit(solution)/shard_map/all_gather | solution.py:45
  125.7 51.7 %fusion.20 = f32[842,4096]{1,0:T(8,128)} fusion(f32[4096,420]{1,0:T(8,128)} %bitcast.71, f32[420,421]{1,0:T(8,128)} %get-tuple-element.6, f32[420,421]{1,0:T(8,128)} %get-tuple-element.7), kind=kOutput, calls=%fused_computation.20 | convolution fusion | flops 17382467584 | bytes 22091168 | tf_op jit(solution)/shard_map/dot_general | solution.py:22
  177.4 0.0 copy-start.4
  177.4 16.8 %copy.9 = f32[106,8,16,256]{3,2,1,0:T(8,128)} copy(f32[106,8,16,256]{3,1,2,0:T(8,128)} %bitcast.70) | data formatting | bytes 27787264
  194.2 0.0 copy-done.4
  194.2 0.0 copy-start.3
  194.2 14.2 %fusion.2 = f32[421,16,4]{1,2,0:T(4,128)} fusion(f32[848,16,256]{2,1,0:T(8,128)} %bitcast.66, f32[256,4,421]{0,1,2:T(4,128)S(1)} %copy-done.4), kind=kOutput, calls=%fused_computation.2 | convolution fusion | flops 82771968 | bytes 15627520 | tf_op jit(solution)/shard_map/spf,rsf->rpf/dot_general | solution.py:32
  208.5 2.1 copy.5
  210.6 0.0 copy-done.3
  210.6 0.0 copy-start.2
  210.6 14.2 %fusion = f32[421,16,4]{1,2,0:T(4,128)} fusion(f32[848,16,256]{2,1,0:T(8,128)} %bitcast.67, f32[256,4,421]{0,1,2:T(4,128)S(1)} %copy-done.3), kind=kOutput, calls=%fused_computation | convolution fusion | flops 82771968 | bytes 15627520 | tf_op jit(solution)/shard_map/spf,rsf->rpf/dot_general | solution.py:32
  224.8 2.1 copy.6
  226.9 0.0 copy-done.2
  226.9 0.0 copy-start.1
  226.9 14.3 %fusion.4 = f32[421,16,4]{1,2,0:T(4,128)} fusion(f32[848,16,256]{2,1,0:T(8,128)} %bitcast.68, f32[256,4,421]{0,1,2:T(4,128)S(1)} %copy-done.2), kind=kOutput, calls=%fused_computation.4 | convolution fusion | flops 82771968 | bytes 15627520 | tf_op jit(solution)/shard_map/spf,rsf->rpf/dot_general | solution.py:32
  241.2 2.1 copy.7
  243.3 0.0 copy-done.1
  243.3 0.0 copy-start.5
  243.3 0.0 copy-start.6
  243.3 14.1 %fusion.6 = f32[421,16,4]{1,2,0:T(4,128)} fusion(f32[848,16,256]{2,1,0:T(8,128)} %bitcast.69, f32[256,4,421]{0,1,2:T(4,128)S(1)} %copy-done.1), kind=kOutput, calls=%fused_computation.6 | convolution fusion | flops 82771968 | bytes 15627520 | tf_op jit(solution)/shard_map/spf,rsf->rpf/dot_general | solution.py:32
  257.4 1.5 copy.8
  258.9 1.0 add_bitcast_fusion
  259.9 0.9 subtract_bitcast_fusion
  260.8 0.0 copy-done.5
  260.8 0.0 copy-done.6
  260.8 2.3 fusion.24
  263.1 0.0 reduce-scatter.2.cloned.1.call-update
  263.1 0.0 copy-done.7
  263.1 0.6 dynamic-slice
  263.7 5.8 %reduce-scatter.2.cloned.1.call-done = f32[8,4,420]{2,0,1:T(8,128)} async-done(((f32[16,4,420]{2,0,1:T(8,128)}), f32[8,4,420]{2,0,1:T(8,128)}) %reduce-scatter.2.cloned.1.call-update) | async-done | bytes 53776 | tf_op jit(solution)/shard_map/reduce_scatter | solution.py:58
  269.5 1.0 multiply_reduce_fusion
  271.1 41.9 %psum.7 = f32[8]{0:T(128)S(1)} all-reduce(f32[8]{0:T(128)S(1)} %multiply_reduce_fusion), channel_id=1, replica_groups=mesh['param'=16,'sensor'=2] {'param'}, use_global_device_ids=true, to_apply=%region_2.3 | all-reduce | flops 8 | bytes 64 | tf_op jit(solution)/shard_map/psum | solution.py:59
  313.0 0.1 fusion.45
  313.1 0.9 broadcast_divide_fusion
  314.0 1.9 all_gather.10
  315.9 0.7 copy.4
  316.7 2.9 all-reduce
  (4 shorter events, 0.0 us)
Async XLA Ops:
  7.2 9.9 %copy-start = (f32[2,256,4,421]{1,2,3,0:T(4,128)S(1)}, f32[2,256,4,421]{1,2,3,0:T(4,128)}, u32[]{:S(2)}) copy-start(f32[2,256,4,421]{1,2,3,0:T(4,128)} %param.3) | copy-start | bytes 10346500
  7.2 118.6 %all-gather.2.cloned.1.call-start = ((), (), s32[]{:S(2)}) async-start(), calls=%async_computation.1 | async-start | bytes 8912896 | tf_op jit(solution)/shard_map/all_gather | solution.py:45
  7.9 261.6 %reduce-scatter.2.cloned.1.call-start = ((), (), s32[]{:S(2)}) async-start(), calls=%async_computation.2 | async-start | bytes 196608 | tf_op jit(solution)/shard_map/reduce_scatter | solution.py:58
  177.4 16.8 %copy-start.4 = (f32[256,4,421]{0,1,2:T(4,128)S(1)}, f32[256,4,421]{0,1,2:T(4,128)}, u32[]{:S(2)}) copy-start(f32[256,4,421]{0,1,2:T(4,128)} %fusion.73) | copy-start | bytes 5173252
  194.2 16.3 %copy-start.3 = (f32[256,4,421]{0,1,2:T(4,128)S(1)}, f32[256,4,421]{0,1,2:T(4,128)}, u32[]{:S(2)}) copy-start(f32[256,4,421]{0,1,2:T(4,128)} %fusion.71) | copy-start | bytes 5173252
  210.6 16.3 %copy-start.2 = (f32[256,4,421]{0,1,2:T(4,128)S(1)}, f32[256,4,421]{0,1,2:T(4,128)}, u32[]{:S(2)}) copy-start(f32[256,4,421]{0,1,2:T(4,128)} %fusion.75) | copy-start | bytes 5173252
  226.9 16.4 %copy-start.1 = (f32[256,4,421]{0,1,2:T(4,128)S(1)}, f32[256,4,421]{0,1,2:T(4,128)}, u32[]{:S(2)}) copy-start(f32[256,4,421]{0,1,2:T(4,128)} %fusion.77) | copy-start | bytes 5173252
  243.3 17.5 %copy-start.5 = (f32[421,420]{0,1:T(8,128)S(1)}, f32[421,420]{0,1:T(8,128)}, u32[]{:S(2)}) copy-start(f32[421,420]{0,1:T(8,128)} %get-tuple-element.8) | copy-start | bytes 2121844
  243.3 17.5 %copy-start.6 = (f32[421,420]{0,1:T(8,128)S(1)}, f32[421,420]{0,1:T(8,128)}, u32[]{:S(2)}) copy-start(f32[421,420]{0,1:T(8,128)} %get-tuple-element.9) | copy-start | bytes 2121844
  257.4 5.7 %copy-start.7 = (u32[32]{0:T(128)S(1)}, u32[32]{0:T(128)}, u32[]{:S(2)}) copy-start(u32[32]{0:T(128)} %constant.35) | copy-start | bytes 388
Sparse Core Ops, SparseCore 0:
  10.8 114.9 all-gather.1
  263.2 6.2 reduce-scatter.1
where the time goes:
time: 330 us; the launch traced here: 327 us
  matrix products  111 us (34%)
  waiting for transfers between devices  109 us (33%)
  blocking collectives  46.8 us (14%)
  local copies, waits for them, and re-layouts  32 us (10%)
  between operations  15 us (5%)
  other arithmetic  13 us (4%)
    all_gather x1, waiting for transfers between devices, body(): lax.all_gather(data, 'param', axis=1, tiled=True)  103 us
    dot_general x4, matrix products, contract(): jnp.einsum('spf,rsf->rpf', kernel, spectrum, precision=lax.Precision.HIGH...  56.8 us
    dot_general x1, matrix products, to_spectrum(): jnp.dot(series.reshape(vectors * sensors, steps), forward, precision=lax....  51.7 us
    psum x1, blocking collectives, body(): squares = lax.psum(jnp.sum(share * share, axis=(1, 2)), 'param')  41.9 us
    unnamed x20, local copies, waits for them, and re-layouts  18.2 us
    dot_general x8, local copies, waits for them, and re-layouts, contract(): jnp.einsum('spf,rsf->rpf', kernel, spectrum, precision=lax.Precision.HIGH...  13.8 us
  transfers between devices with their start and end apart: 2, of which 2 were waited for; matrix products, arithmetic and copies ran while one was open for 5% of the time, Pallas kernels for 0%

commit v1 on v0

--- a/solution.py
+++ b/solution.py
@@ -42,7 +42,7 @@
     steps = data.shape[2]
     freqs = steps + 1
     forward, backward = spectral_tables(steps)
-    whole = to_spectrum(lax.all_gather(data, "param", axis=1, tiled=True), forward)
+    whole = to_spectrum(jnp.concatenate(lax.all_gather(data, "param"), axis=1), forward)
     real_part = whole[..., :freqs]
     imag_part = whole[..., freqs:]
     kernel_re = spectra[0]

time: 330 us -> 313 us (0.948)
  matrix products: 111 us -> 97.3 us
    dot_general x4, matrix products: 56.8 us -> 45.5 us  [contract(): jnp.einsum('spf,rsf->rpf', kernel, spectrum, precision=lax.Precision.HIGH...]
    dot_general x8 -> x4, local copies, waits for them, and re-layouts: 13.8 us -> 6.04 us  [contract(): jnp.einsum('spf,rsf->rpf', kernel, spectrum, precision=lax.Precision.HIGH...]
    all_gather x0 -> x1, local copies, waits for them, and re-layouts: none -> 4.57 us  [body(): lax.all_gather(data, 'param')]
    unnamed x20 -> x26, local copies, waits for them, and re-layouts: 18.2 us -> 18.2 us
where the time goes in v1:
time: 313 us; the launch traced here: 309 us
  waiting for transfers between devices  109 us (35%)
  matrix products  97.3 us (31%)
  blocking collectives  46.8 us (15%)
  local copies, waits for them, and re-layouts  30.1 us (10%)
  between operations  15.1 us (5%)
  other arithmetic  11 us (4%)
    all_gather x1, waiting for transfers between devices, body(): lax.all_gather(data, 'param')  103 us
    dot_general x1, matrix products, to_spectrum(): jnp.dot(series.reshape(vectors * sensors, steps), forward, precision=lax....  49.6 us
    dot_general x4, matrix products, contract(): jnp.einsum('spf,rsf->rpf', kernel, spectrum, precision=lax.Precision.HIGH...  45.5 us
    psum x1, blocking collectives, body(): squares = lax.psum(jnp.sum(share * share, axis=(1, 2)), 'param')  41.9 us
    unnamed x26, local copies, waits for them, and re-layouts  18.2 us
  transfers between devices with their start and end apart: 2, of which 2 were waited for; matrix products, arithmetic and copies ran while one was open for 5% of the time, Pallas kernels for 0%

profile of v1, /device:TPU:0, one launch (start us, length us, event | category | flops | bytes accessed | tf_op | source)
XLA Modules:
  0.0 309.1 jit_solution(1585148342669971536)
XLA Ops:
  7.2 0.0 copy-start
  7.2 0.0 all-gather.3.cloned.1.call-start
  7.2 0.7 all-gather.3.cloned.1.call-update
  7.9 0.0 reduce-scatter.2.cloned.1.call-start
  8.0 4.5 %sine_negate_fusion = (f32[420,421]{1,0:T(8,128)}, f32[420,421]{1,0:T(8,128)}) fusion(), kind=kLoop, calls=%fused_computation.43 | loop fusion | flops 1768200 | bytes 1414560 | tf_op jit(solution)/shard_map/neg | solution.py:14
  12.5 4.5 %sine_multiply_fusion = (f32[421,420]{0,1:T(8,128)}, f32[421,420]{0,1:T(8,128)}) fusion(f32[421]{0:T(512)S(1)} %fusion.62, f32[421]{0:T(512)S(1)} %select_multiply_fusion), kind=kLoop, calls=%fused_computation.38 | loop fusion | flops 1945020 | bytes 1417928 | tf_op jit(solution)/shard_map/mul | solution.py:16
  17.0 0.0 copy-done
  17.0 1.5 fusion.91
  18.5 1.5 fusion.97
  20.0 1.5 fusion.93
  21.5 1.5 fusion.95
  23.1 102.7 %all-gather.3.cloned.1.call-done = f32[256,16,420]{2,1,0:T(8,128)} async-done(((f32[16,16,420]{2,1,0:T(8,128)}), f32[256,16,420]{2,1,0:T(8,128)}) %all-gather.3.cloned.1.call-update) | async-done | bytes 6881296 | tf_op jit(solution)/shard_map/all_gather | solution.py:45
  125.8 4.6 %copy.10 = f32[16,16,16,420]{3,2,0,1:T(8,128)S(1)} copy(f32[16,16,16,420]{3,2,1,0:T(8,128)} %bitcast.95) | data formatting | bytes 13762560 | tf_op jit(solution)/shard_map/all_gather | solution.py:45
  130.4 0.0 copy-done.7
  130.4 0.0 copy-done.8
  130.4 49.6 %fusion.20 = f32[842,4096]{1,0:T(8,128)} fusion(f32[4096,420]{1,0:T(8,128)S(1)} %bitcast.94, f32[420,421]{1,0:T(8,128)S(1)} %copy-done.7, f32[420,421]{1,0:T(8,128)S(1)} %copy-done.8), kind=kOutput, calls=%fused_computation.20 | convolution fusion | flops 17382467584 | bytes 22091168 | tf_op jit(solution)/shard_map/dot_general | solution.py:22
  180.0 0.0 copy-start.4
  180.0 16.8 %copy.14 = f32[106,8,16,256]{3,2,1,0:T(8,128)} copy(f32[106,8,16,256]{3,1,2,0:T(8,128)} %bitcast.93) | data formatting | bytes 27787264
  196.8 0.0 copy-done.4
  196.8 13.3 %fusion = f32[421,16,4]{1,2,0:T(4,128)S(1)} fusion(f32[848,16,256]{2,1,0:T(8,128)} %bitcast.89, f32[256,4,421]{0,1,2:T(4,128)S(1)} %copy-done.4), kind=kOutput, calls=%fused_computation | convolution fusion | flops 82771968 | bytes 15627520 | tf_op jit(solution)/shard_map/spf,rsf->rpf/dot_general | solution.py:32
  210.1 0.0 copy-done.3
  210.1 0.0 copy-start.2
  210.1 9.5 %fusion.42 = f32[16,4,421]{0,1,2:T(4,128)S(1)} fusion(f32[421,16,4]{1,2,0:T(4,128)S(1)} %fusion, f32[848,16,256]{2,1,0:T(8,128)} %bitcast.90, f32[256,4,421]{0,1,2:T(4,128)S(1)} %copy-done.3), kind=kOutput, calls=%fused_computation.31 | convolution fusion | flops 82798912 | bytes 15735296 | tf_op jit(solution)/shard_map/spf,rsf->rpf/dot_general | solution.py:32
  219.6 1.0 copy.11
  220.6 0.0 copy-done.2
  220.6 13.3 %fusion.4 = f32[421,16,4]{1,2,0:T(4,128)S(1)} fusion(f32[848,16,256]{2,1,0:T(8,128)} %bitcast.91, f32[256,4,421]{0,1,2:T(4,128)S(1)} %copy-done.2), kind=kOutput, calls=%fused_computation.4 | convolution fusion | flops 82771968 | bytes 15627520 | tf_op jit(solution)/shard_map/spf,rsf->rpf/dot_general | solution.py:32
  233.9 0.0 copy-done.1
  233.9 0.0 copy-start.5
  233.9 0.0 copy-start.6
  233.9 0.0 copy-start.9
  234.0 0.0 copy-start.10
  234.0 9.4 %fusion.32 = f32[16,4,421]{0,1,2:T(4,128)S(1)} fusion(f32[421,16,4]{1,2,0:T(4,128)S(1)} %fusion.4, f32[848,16,256]{2,1,0:T(8,128)} %bitcast.92, f32[256,4,421]{0,1,2:T(4,128)S(1)} %copy-done.1), kind=kOutput, calls=%fused_computation.29 | convolution fusion | flops 82798912 | bytes 15735296 | tf_op jit(solution)/shard_map/spf,rsf->rpf/dot_general | solution.py:32
  243.4 0.3 copy.12
  243.7 0.0 copy-done.5
  243.7 0.0 copy-done.6
  243.7 0.0 copy-done.9
  243.7 2.3 fusion.24
  246.0 0.0 reduce-scatter.2.cloned.1.call-update
  246.0 0.0 copy-done.10
  246.0 0.6 dynamic-slice
  246.6 5.3 %reduce-scatter.2.cloned.1.call-done = f32[8,4,420]{2,0,1:T(8,128)} async-done(((f32[16,4,420]{2,0,1:T(8,128)}), f32[8,4,420]{2,0,1:T(8,128)}) %reduce-scatter.2.cloned.1.call-update) | async-done | bytes 53776 | tf_op jit(solution)/shard_map/reduce_scatter | solution.py:58
  251.9 1.0 multiply_reduce_fusion
  253.6 41.9 %psum.7 = f32[8]{0:T(128)S(1)} all-reduce(f32[8]{0:T(128)S(1)} %multiply_reduce_fusion), channel_id=1, replica_groups=mesh['param'=16,'sensor'=2] {'param'}, use_global_device_ids=true, to_apply=%region_2.3 | all-reduce | flops 8 | bytes 64 | tf_op jit(solution)/shard_map/psum | solution.py:59
  295.5 0.1 fusion.65
  295.6 0.9 broadcast_divide_fusion
  296.5 1.9 all_gather.14
  298.4 0.7 copy.13
  299.1 2.9 all-reduce
  (7 shorter events, 0.0 us)
Async XLA Ops:
  7.2 9.9 %copy-start = (f32[2,256,4,421]{1,2,3,0:T(4,128)S(1)}, f32[2,256,4,421]{1,2,3,0:T(4,128)}, u32[]{:S(2)}) copy-start(f32[2,256,4,421]{1,2,3,0:T(4,128)} %param.3) | copy-start | bytes 10346500
  7.2 118.6 %all-gather.3.cloned.1.call-start = ((), (), s32[]{:S(2)}) async-start(), calls=%async_computation.2 | async-start | bytes 8912896 | tf_op jit(solution)/shard_map/all_gather | solution.py:45
  7.9 244.0 %reduce-scatter.2.cloned.1.call-start = ((), (), s32[]{:S(2)}) async-start(), calls=%async_computation.1 | async-start | bytes 196608 | tf_op jit(solution)/shard_map/reduce_scatter | solution.py:58
  125.8 4.6 %copy-start.7 = (f32[420,421]{1,0:T(8,128)S(1)}, f32[420,421]{1,0:T(8,128)}, u32[]{:S(2)}) copy-start(f32[420,421]{1,0:T(8,128)} %get-tuple-element.12) | copy-start | bytes 2121844
  125.8 4.6 %copy-start.8 = (f32[420,421]{1,0:T(8,128)S(1)}, f32[420,421]{1,0:T(8,128)}, u32[]{:S(2)}) copy-start(f32[420,421]{1,0:T(8,128)} %get-tuple-element.13) | copy-start | bytes 2121844
  180.0 16.8 %copy-start.4 = (f32[256,4,421]{0,1,2:T(4,128)S(1)}, f32[256,4,421]{0,1,2:T(4,128)}, u32[]{:S(2)}) copy-start(f32[256,4,421]{0,1,2:T(4,128)} %fusion.91) | copy-start | bytes 5173252
  196.8 13.3 %copy-start.3 = (f32[256,4,421]{0,1,2:T(4,128)S(1)}, f32[256,4,421]{0,1,2:T(4,128)}, u32[]{:S(2)}) copy-start(f32[256,4,421]{0,1,2:T(4,128)} %fusion.97) | copy-start | bytes 5173252
  210.1 10.5 %copy-start.2 = (f32[256,4,421]{0,1,2:T(4,128)S(1)}, f32[256,4,421]{0,1,2:T(4,128)}, u32[]{:S(2)}) copy-start(f32[256,4,421]{0,1,2:T(4,128)} %fusion.93) | copy-start | bytes 5173252
  220.6 13.3 %copy-start.1 = (f32[256,4,421]{0,1,2:T(4,128)S(1)}, f32[256,4,421]{0,1,2:T(4,128)}, u32[]{:S(2)}) copy-start(f32[256,4,421]{0,1,2:T(4,128)} %fusion.95) | copy-start | bytes 5173252
  233.9 9.8 %copy-start.5 = (f32[421,420]{0,1:T(8,128)S(1)}, f32[421,420]{0,1:T(8,128)}, u32[]{:S(2)}) copy-start(f32[421,420]{0,1:T(8,128)} %get-tuple-element.14) | copy-start | bytes 2121844
  233.9 9.8 %copy-start.6 = (f32[421,420]{0,1:T(8,128)S(1)}, f32[421,420]{0,1:T(8,128)}, u32[]{:S(2)}) copy-start(f32[421,420]{0,1:T(8,128)} %get-tuple-element.15) | copy-start | bytes 2121844
  233.9 9.8 %copy-start.9 = (f32[16,4,421]{2,0,1:T(8,128)S(1)}, f32[16,4,421]{2,0,1:T(8,128)}, u32[]{:S(2)}) copy-start(f32[16,4,421]{2,0,1:T(8,128)} %copy.11) | copy-start | bytes 323332
  234.0 12.1 %copy-start.10 = (u32[32]{0:T(128)S(1)}, u32[32]{0:T(128)}, u32[]{:S(2)}) copy-start(u32[32]{0:T(128)} %constant.35) | copy-start | bytes 388
Sparse Core Ops, SparseCore 0:
  10.8 115.0 all-gather.2
  246.2 5.7 reduce-scatter.1
